TPU v7x, 32 devices: a whole 2x2x4 slice. The times are simulated.
32 devices in a mesh: pts: 8 (over y, x, core), cand: 4 (over z).
Axes of the slice: x: 2, y: 2, z: 4, core: 2. Of those that a mesh axis runs over, the one named last changes fastest.
Arguments:
- points: bfloat16 [8192, 1024], P('pts'), may hold values from -6 to 6
- weights: float32 [8192], P('pts'), may hold values from 0.5 to 5
- coverage: float32 [8192], P('pts'), may hold values from -0.5 to 1
- candidates: bfloat16 [4096, 1024], P('cand'), may hold values from -6 to 6
- picks: int32 [64], replicated, may hold values from 0 to 4095
Outputs:
- gains: float32 [4096], P('cand')
- top_gains: float32 [64], replicated
- new_coverage: float32 [8192], P('pts')
All inputs are finite; a program needn't handle non-finite values.
Results may differ from a plain program's by a relative error of at most 0.0003.
Values may be sent and summed in bfloat16 or wider, within the bound.
A program may use at most 64 MiB of HBM per device.

v0:
```python
import functools

import jax
import jax.numpy as jnp
from jax import lax
from jax.experimental import pallas as pl
from jax.experimental.pallas import tpu as pltpu
from jax.sharding import PartitionSpec as P

TOPK = 64
LANES = 128
MESH = pl.DeviceIdType.MESH
F32 = jnp.float32
LOW = -1e30
HIGH = 3e38
CHUNK = 512


def column_tile(row):
    return jnp.transpose(jnp.broadcast_to(row, (LANES, LANES)))


def ranked(columns, rows, count):
    wide = [jnp.broadcast_to(row, (8, LANES)) for row in rows]
    above = [jnp.zeros((8, LANES), F32) for _ in rows]
    for column in columns:
        for g in range(column.shape[0] // 8):
            value = column[g * 8 : (g + 1) * 8, :]
            above = [a + jnp.where(value > w, 1.0, 0.0) for a, w in zip(above, wide)]
    place = lax.broadcasted_iota(jnp.int32, (count, LANES), 0).astype(F32)
    best = jnp.full((count, LANES), HIGH, F32)
    for a, row in zip(above, rows):
        total = jnp.sum(a, axis=0, keepdims=True)
        best = jnp.minimum(best, jnp.where(total <= place, row, HIGH))
    return jnp.min(best, axis=1, keepdims=True)


def as_row(column):
    count = column.shape[0]
    wide = jnp.broadcast_to(column, (count, LANES))
    if count < LANES:
        wide = jnp.concatenate([wide, jnp.full((LANES - count, LANES), -1.0, F32)], axis=0)
    return jnp.transpose(wide)[0:1, :]


def kernel(
    n_pts, n_cand, points, weights, coverage, candidates, picks, gains_out, lists_out, cover_out,
    p_buf, c_buf, w_buf, v_buf, k_buf, w_col, v_col, g_acc, b_acc, part, parts, best, bests,
    top, tops, g_col, in_sem, small_sem, part_send, part_recv, best_send, best_recv, top_send, top_recv,
    spoken,
):
    rows, depth = points.shape
    cands = candidates.shape[0]
    me, mz = lax.axis_index("pts"), lax.axis_index("cand")
    n_p, n_c = rows // CHUNK, cands // CHUNK
    tiles_p, tiles_c = rows // LANES, cands // LANES
    scale = depth ** (-0.5)

    small = [
        pltpu.make_async_copy(weights, w_buf, small_sem.at[0]),
        pltpu.make_async_copy(coverage, v_buf, small_sem.at[1]),
        pltpu.make_async_copy(picks, k_buf, small_sem.at[2]),
    ]
    for copy in small:
        copy.start()
    barrier = pltpu.get_barrier_semaphore()
    for k in range(1, n_cand):
        other = lax.rem(mz + k, n_cand)
        pl.semaphore_signal(barrier, inc=1, device_id={"cand": other}, device_id_type=MESH)
        pl.semaphore_signal(
            barrier, inc=1, device_id={"pts": n_pts - 1, "cand": other}, device_id_type=MESH
        )

    loads = {}
    order = []
    for i in range(max(n_p, n_c)):
        if i < n_c:
            order.append(("c", i))
        if i < n_p:
            order.append(("p", i))
    for at, (kind, i) in enumerate(order):
        src, dst = (points, p_buf) if kind == "p" else (candidates, c_buf)
        span = pl.ds(i * CHUNK, CHUNK)
        loads[kind, i] = pltpu.make_async_copy(src.at[span, :], dst.at[span, :], in_sem.at[at])
        loads[kind, i].start()

    for k in range(1, n_pts):
        pl.semaphore_signal(
            barrier, inc=1, device_id={"pts": lax.rem(me + k, n_pts)}, device_id_type=MESH
        )

    for copy in small:
        copy.wait()
    column = mz * cands + lax.broadcasted_iota(jnp.int32, (tiles_c, LANES), 0) * LANES
    column = column + lax.broadcasted_iota(jnp.int32, (tiles_c, LANES), 1)
    chosen = jnp.zeros((tiles_c, LANES), jnp.bool_)
    for k in range(picks.shape[0]):
        chosen = chosen | (column == k_buf[k])
    penalty = jnp.where(chosen, 0.0, LOW)
    w_row = w_buf[...] * (scale / (rows * n_pts))
    v_row = v_buf[...] * (1.0 / scale)
    for t in range(tiles_p):
        w_col[t * LANES : (t + 1) * LANES, :] = column_tile(w_row[t : t + 1, :])
        v_col[t * LANES : (t + 1) * LANES, :] = column_tile(v_row[t : t + 1, :])

    def block(p_from, p_to, c_from, c_to):
        ps, many = pl.ds(p_from, p_to - p_from), p_to - p_from
        sims = lax.dot_general(
            p_buf[ps, :], c_buf[pl.ds(c_from, c_to - c_from), :],
            (((1,), (1,)), ((), ())), preferred_element_type=F32,
        )
        w, v = w_col[ps, :], v_col[ps, :]
        found = None
        for tile in range(c_from // LANES, c_to // LANES):
            lanes = slice(tile * LANES, (tile + 1) * LANES)
            x = sims[:, tile * LANES - c_from : (tile + 1) * LANES - c_from]
            value = jnp.maximum(x - v, 0.0) * w
            value = jnp.sum(value.reshape(many // 8, 8, LANES), axis=0)
            if p_from == 0:
                g_acc[:, lanes] = value
            else:
                g_acc[:, lanes] += value
            x = x + penalty[tile : tile + 1, :]
            found = x if found is None else jnp.maximum(found, x)
        if c_from == 0:
            b_acc[ps, :] = found
        else:
            b_acc[ps, :] = jnp.maximum(b_acc[ps, :], found)

    here_p = here_c = 0
    for kind, i in order:
        loads[kind, i].wait()
        if kind == "p":
            here_p += CHUNK
            if here_c:
                block(here_p - CHUNK, here_p, 0, here_c)
        else:
            here_c += CHUNK
            if here_p:
                block(0, here_p, here_c - CHUNK, here_c)

    for t in range(tiles_c):
        part[t : t + 1, :] = jnp.sum(g_acc[:, t * LANES : (t + 1) * LANES], axis=0, keepdims=True)

    speaks = me == n_pts - 1
    greetings = n_pts - 1 + n_cand - 1
    pl.semaphore_wait(barrier, jnp.where(speaks, greetings + n_pts * (n_cand - 1), greetings))

    def exchange(axis, n, mine, src, slots, send, recv):
        for k in range(1, n):
            pltpu.make_async_remote_copy(
                src_ref=src, dst_ref=slots.at[mine], send_sem=send.at[0], recv_sem=recv.at[0],
                device_id={axis: lax.rem(mine + k, n)}, device_id_type=MESH,
            ).start()

    def settle(slots, n, sem):
        view = slots.at[pl.ds(0, n)]
        pltpu.make_async_copy(view, view, sem.at[0]).wait()

    exchange("pts", n_pts, me, part, parts, part_send, part_recv)
    parts[me] = part[...]

    def cover_exchange():
        for t in range(tiles_p):
            turned = jnp.transpose(b_acc[t * LANES : (t + 1) * LANES, :])
            best[t : t + 1, :] = jnp.max(turned, axis=0, keepdims=True)
        exchange("cand", n_cand, mz, best, bests, best_send, best_recv)

    pl.when(jnp.logical_not(speaks))(cover_exchange)

    settle(parts, n_pts - 1, part_recv)
    gains = parts[0]
    for k in range(1, n_pts):
        gains = gains + parts[k]
    gains_out[...] = gains

    for t in range(tiles_c):
        g_col[t * LANES : (t + 1) * LANES, :] = column_tile(gains[t : t + 1, :])
    sorted_col = ranked([g_col], [gains[t : t + 1, :] for t in range(tiles_c)], TOPK)
    top_row = as_row(sorted_col)
    top[...] = top_row

    def announce(k, p):
        return pltpu.make_async_remote_copy(
            src_ref=top, dst_ref=tops.at[mz], send_sem=top_send.at[0], recv_sem=top_recv.at[0],
            device_id={"pts": p, "cand": lax.rem(mz + k, n_cand)}, device_id_type=MESH,
        )

    @pl.when(speaks)
    def _():
        for p in range(n_pts):
            for k in range(1, n_cand):
                announce(k, p).start()
        cover_exchange()

    tops[mz] = top_row

    settle(bests, n_cand - 1, best_recv)
    cover = best[...]
    for k in range(1, n_cand):
        cover = jnp.maximum(cover, bests[lax.rem(mz + k, n_cand)])
    cover_out[...] = jnp.maximum(v_buf[...], cover * scale)

    settle(tops, n_cand - 1, top_recv)
    for k in range(n_cand):
        lists_out[k : k + 1, :] = tops[k]

    settle(parts, n_pts - 1, part_send)
    settle(bests, n_cand - 1, best_send)

    @pl.when(speaks)
    def _():
        settle(spoken, n_pts * (n_cand - 1), top_send)


def finish(gains, lists, cover, gains_out, top_out, cover_out, sems, top_buf):
    gains_copy = pltpu.make_async_copy(gains, gains_out, sems.at[0])
    cover_copy = pltpu.make_async_copy(cover, cover_out, sems.at[1])
    gains_copy.start()
    cover_copy.start()
    rows = [lists[k : k + 1, :] for k in range(lists.shape[0])]
    merged = ranked([column_tile(row)[:TOPK, :] for row in rows], rows, TOPK)
    top_buf[...] = as_row(merged)[:, :TOPK]
    top_copy = pltpu.make_async_copy(top_buf, top_out, sems.at[2])
    top_copy.start()
    gains_copy.wait()
    cover_copy.wait()
    top_copy.wait()


def solution(mesh):
    n_pts, n_cand = mesh.shape["pts"], mesh.shape["cand"]

    def on_device(points, weights, coverage, candidates, picks):
        rows, depth = points.shape
        cands = candidates.shape[0]
        tp, tc = rows // LANES, cands // LANES
        anywhere = pl.BlockSpec(memory_space=pl.ANY)
        dma = pltpu.SemaphoreType.DMA
        vmem = pltpu.VMEM
        gains, lists, cover = pl.pallas_call(
            functools.partial(kernel, n_pts, n_cand),
            out_shape=(
                vmem((tc, LANES), F32),
                vmem((n_cand, LANES), F32),
                vmem((tp, LANES), F32),
            ),
            in_specs=[anywhere] * 5,
            out_specs=(pl.BlockSpec(memory_space=vmem),) * 3,
            scratch_shapes=[
                vmem((rows, depth), points.dtype), vmem((cands, depth), candidates.dtype),
                vmem((tp, LANES), F32), vmem((tp, LANES), F32),
                pltpu.SMEM(picks.shape, jnp.int32),
                vmem((rows, LANES), F32), vmem((rows, LANES), F32),
                vmem((8, cands), F32), vmem((rows, LANES), F32),
                vmem((tc, LANES), F32), vmem((n_pts, tc, LANES), F32),
                vmem((tp, LANES), F32), vmem((n_cand, tp, LANES), F32),
                vmem((1, LANES), F32), vmem((n_cand, 1, LANES), F32),
                vmem((cands, LANES), F32),
                dma((rows // CHUNK + cands // CHUNK,)), dma((3,)),
                dma((1,)), dma((1,)), dma((1,)), dma((1,)), dma((1,)), dma((1,)),
                vmem((n_pts * (n_cand - 1), 1, LANES), F32),
            ],
            compiler_params=pltpu.CompilerParams(
                collective_id=0, has_side_effects=True, vmem_limit_bytes=60 * 2**20
            ),
            name="facility",
        )(points, weights.reshape(tp, LANES), coverage.reshape(tp, LANES), candidates, picks)
        gains, top, cover = pl.pallas_call(
            finish,
            out_shape=(
                jax.ShapeDtypeStruct((tc, LANES), F32),
                jax.ShapeDtypeStruct((1, TOPK), F32),
                jax.ShapeDtypeStruct((tp, LANES), F32),
            ),
            in_specs=[pl.BlockSpec(memory_space=vmem)] * 3,
            out_specs=(anywhere,) * 3,
            scratch_shapes=[dma((3,)), vmem((1, TOPK), F32)],
            name="finish",
        )(*(pltpu.with_memory_space_constraint(x, vmem) for x in (gains, lists, cover)))
        return gains.reshape(cands), top.reshape(TOPK), cover.reshape(rows)

    placed = (P("pts", None), P("pts"), P("pts"), P("cand", None), P())
    return jax.shard_map(
        on_device, mesh=mesh, in_specs=placed, out_specs=(P("cand"), P(), P("pts")), check_vma=False
    )
```

profile of v0, /device:TPU:0, one launch (start us, length us, event | category | flops | bytes accessed | tf_op | source)
XLA Modules:
  0.0 17.0 jit_solution(8394084340165158328)
XLA Ops:
  0.6 15.6 %facility.1 = (f32[8,128]{1,0:T(8,128)S(1)}, f32[4,128]{1,0:T(4,128)S(1)}, f32[8,128]{1,0:T(8,128)S(1)}) custom-call(bf16[1024,1024]{1,0:T(8,128)(2,1)} %points.1, f32[8,128]{1,0:T(8,128)} %bitcast.5, f32[8,128]{1,0:T(8,128)} %bitcast.6, bf16[1024,1024]{1,0:T(8,128)(2,1)} %candidates.1, s32[64]{0:T(128)} %picks.1), custom_call_target="tpu_custom_call" | custom-call | tf_op jit(solution)/shard_map/facility/pallas_call | solution.py:241
  16.2 0.8 %finish.1 = (f32[8,128]{1,0:T(8,128)}, f32[1,64]{1,0:T(1,128)}, f32[8,128]{1,0:T(8,128)}) custom-call(f32[8,128]{1,0:T(8,128)S(1)} %get-tuple-element.9.gains, f32[4,128]{1,0:T(4,128)S(1)} %get-tuple-element.10.lists, f32[8,128]{1,0:T(8,128)S(1)} %get-tuple-element.11.cover), custom_call_target="tpu_custom_call" | custom-call | tf_op jit(solution)/shard_map/finish/pallas_call | solution.py:269
where the time goes:
time: 17.2 us; the launch traced here: 17 us
  Pallas kernels  16.4 us (95%)
  between operations  0.64 us (4%)
    pallas_call x1, Pallas kernels, on_device(): pl.pallas_call(functools.partial(kernel, n_pts, n_cand), out_shape=(vmem(...  15.6 us
    pallas_call x1, Pallas kernels, on_device(): pl.pallas_call(finish, out_shape=(jax.ShapeDtypeStruct((tc, LANES), F32),...  0.82 us

commit v1 on v0

v1 whole, which is shorter than its diff:
```python
import functools

import jax
import jax.numpy as jnp
from jax import lax
from jax.experimental import pallas as pl
from jax.experimental.pallas import tpu as pltpu
from jax.sharding import PartitionSpec as P

TOPK = 64
LANES = 128
MESH = pl.DeviceIdType.MESH
F32 = jnp.float32
LOW = -1e30
HIGH = 3e38
HALF = 512
WIDE = 256
STEP = 64


def column_tile(row):
    return jnp.transpose(jnp.broadcast_to(row, (LANES, LANES)))


def kernel(
    n_pts, n_cand, points, weights, coverage, candidates, picks, gains_out, top_out, cover_out,
    p_buf, c_buf, w_buf, v_buf, k_buf, w_col, v_col, b_acc, part_a, part_b, parts_a, parts_b,
    best, bests, all_gains, n_col, t_col, top_row, got_gains, got_top,
    in_sem, small_sem, a_send, a_recv, b_send, b_recv, best_send, best_recv,
    gain_send, gain_recv, top_send, top_recv, sent,
):
    rows, depth = points.shape
    cands = candidates.shape[0]
    me, mz = lax.axis_index("pts"), lax.axis_index("cand")
    n_p, n_c = rows // HALF, cands // WIDE
    tiles_p, tiles_c = rows // LANES, cands // LANES
    tiles_w = WIDE // LANES
    rows_b = tiles_w
    rows_a = tiles_c - rows_b
    pair = 2 if n_pts % 2 == 0 else 1
    scale = depth ** (-0.5)

    loads = {}
    order = [("c", 0), ("p", 0)] + [("p", i) for i in range(1, n_p)] + [("c", i) for i in range(1, n_c)]
    for at, (kind, i) in enumerate(order):
        src, dst, size = (points, p_buf, HALF) if kind == "p" else (candidates, c_buf, WIDE)
        span = pl.ds(i * size, size)
        loads[kind, i] = pltpu.make_async_copy(src.at[span, :], dst.at[span, :], in_sem.at[at])
    small = [
        pltpu.make_async_copy(weights, w_buf, small_sem.at[0]),
        pltpu.make_async_copy(coverage, v_buf, small_sem.at[1]),
        pltpu.make_async_copy(picks, k_buf, small_sem.at[2]),
    ]
    for copy in small:
        copy.start()
    for key in order:
        loads[key].start()

    base = mz == 0
    relay = me // pair * pair + pair - 1
    speaks = base & (me == relay)
    barrier = pltpu.get_barrier_semaphore()

    def greet(p, z):
        pl.semaphore_signal(barrier, inc=1, device_id={"pts": p, "cand": z}, device_id_type=MESH)

    @pl.when(base)
    def _():
        for z in range(n_cand):
            for k in range(n_pts):
                if z == 0 and k == 0:
                    continue
                greet(lax.rem(me + k, n_pts), z)

    for k in range(1, n_cand):
        greet(me, lax.rem(mz + k, n_cand))

    @pl.when(jnp.logical_not(base))
    def _():
        greet(relay, 0)

    for copy in small:
        copy.wait()
    w_row = w_buf[...] * (scale / (rows * n_pts))
    v_row = v_buf[...] * (1.0 / scale)
    for t in range(tiles_p):
        w_col[t * LANES : (t + 1) * LANES, :] = column_tile(w_row[t : t + 1, :])
        v_col[t * LANES : (t + 1) * LANES, :] = column_tile(v_row[t : t + 1, :])
    column = mz * cands + lax.broadcasted_iota(jnp.int32, (tiles_c, LANES), 0) * LANES
    column = column + lax.broadcasted_iota(jnp.int32, (tiles_c, LANES), 1)
    chosen = jnp.zeros((tiles_c, LANES), jnp.bool_)
    for k in range(picks.shape[0]):
        chosen = chosen | (column == k_buf[k])
    penalty = jnp.where(chosen, 0.0, LOW)

    def dot(p_from, many, c):
        return lax.dot_general(
            p_buf[p_from : p_from + many, :], c_buf[c * WIDE : (c + 1) * WIDE, :],
            (((1,), (1,)), ((), ())), preferred_element_type=F32,
        )

    def epilogue(sims, p_from, c, sums):
        many = sims.shape[0]
        for r in range(0, many, STEP):
            at = slice(p_from + r, p_from + r + STEP)
            w, v = w_col[at, :], v_col[at, :]
            found = b_acc[at, :] if c else None
            for t in range(tiles_w):
                x = sims[r : r + STEP, t * LANES : (t + 1) * LANES]
                value = jnp.maximum(x - v, 0.0) * w
                value = jnp.sum(value.reshape(STEP // 8, 8, LANES), axis=0)
                sums[t] = value if sums[t] is None else sums[t] + value
                tile = c * tiles_w + t
                x = x + penalty[tile : tile + 1, :]
                found = x if found is None else jnp.maximum(found, x)
            b_acc[at, :] = found

    def settle_sums(sums, dst, c):
        for t in range(tiles_w):
            dst[c * tiles_w + t : c * tiles_w + t + 1, :] = jnp.sum(sums[t], axis=0, keepdims=True)

    def send_parts(src, slots, send, recv):
        def to(p):
            pltpu.make_async_remote_copy(
                src_ref=src, dst_ref=slots.at[mz, me], send_sem=send.at[0], recv_sem=recv.at[mz],
                device_id={"pts": p, "cand": 0}, device_id_type=MESH,
            ).start()

        @pl.when(jnp.logical_not(base))
        def _():
            for p in range(n_pts):
                to(p)

        @pl.when(base)
        def _():
            for k in range(1, n_pts):
                to(lax.rem(me + k, n_pts))
            slots[0, me] = src[...]

    work = []
    for i in range(n_p):
        work.append((i * HALF, HALF, 0, ("p", i)))
    for c in range(1, n_c):
        work.append((0, rows, c, ("c", c)))
    loads["c", 0].wait()
    sums = [None] * tiles_w
    held = None
    for at, (p_from, many, c, key) in enumerate(work):
        loads[key].wait()
        sims = dot(p_from, many, c)
        if held is not None:
            epilogue(*held, sums)
            if held[2] != c:
                settle_sums(sums, part_a, held[2])
                sums = [None] * tiles_w
        held = (sims, p_from, c)

    greetings = (n_cand - 1) + n_pts
    awaited = jnp.where(base, greetings - 1, greetings)
    awaited = awaited + jnp.where(speaks, pair * (n_cand - 1), 0)
    pl.semaphore_wait(barrier, awaited)
    send_parts(part_a, parts_a, a_send, a_recv)
    epilogue(*held, sums)
    settle_sums(sums, part_b, 0)
    send_parts(part_b, parts_b, b_send, b_recv)

    for t in range(tiles_p):
        turned = jnp.transpose(b_acc[t * LANES : (t + 1) * LANES, :])
        best[t : t + 1, :] = jnp.max(turned, axis=0, keepdims=True)
    for k in range(1, n_cand):
        pltpu.make_async_remote_copy(
            src_ref=best, dst_ref=bests.at[mz], send_sem=best_send.at[0], recv_sem=best_recv.at[0],
            device_id={"cand": lax.rem(mz + k, n_cand)}, device_id_type=MESH,
        ).start()

    def settle(view, sem):
        pltpu.make_async_copy(view, view, sem).wait()

    def finish_cover():
        settle(bests.at[pl.ds(0, n_cand - 1)], best_recv.at[0])
        cover = best[...]
        for k in range(1, n_cand):
            cover = jnp.maximum(cover, bests[lax.rem(mz + k, n_cand)])
        cover_out[...] = jnp.maximum(v_buf[...], cover * scale)
        settle(bests.at[pl.ds(0, n_cand - 1)], best_send.at[0])

    place = lax.broadcasted_iota(jnp.int32, (8, LANES), 1).astype(F32)
    lane = lax.broadcasted_iota(jnp.int32, (1, LANES), 1)

    def merge(new):
        for i, row in enumerate(new):
            n_col[i * LANES : (i + 1) * LANES, :] = column_tile(row)
        across = [jnp.broadcast_to(row, (8, LANES)) for row in new]
        across.append(jnp.broadcast_to(top_row[...], (8, LANES)))
        columns = [t_col[g * 8 : (g + 1) * 8, :] for g in range(TOPK // 8)]
        columns += [n_col[g * 8 : (g + 1) * 8, :] for g in range(len(new) * LANES // 8)]
        kept = jnp.full((8, LANES), HIGH, F32)
        for column in columns:
            above = jnp.zeros((8, LANES), F32)
            for row in across:
                above = above + jnp.where(row > column, 1.0, 0.0)
            above = jnp.sum(above, axis=1, keepdims=True)
            kept = jnp.minimum(kept, jnp.where(above <= place, column, HIGH))
        kept = jnp.min(kept, axis=0, keepdims=True)
        return jnp.where(lane < TOPK, kept, LOW)

    def told(z, k, src, dst, send, recv):
        return pltpu.make_async_remote_copy(
            src_ref=src, dst_ref=dst, send_sem=send.at[0], recv_sem=recv.at[0],
            device_id={"pts": me - pair + 1 + k, "cand": z}, device_id_type=MESH,
        )

    @pl.when(base)
    def _():
        top_row[...] = jnp.where(lane < TOPK, -1.0, LOW)
        for z in range(n_cand):
            count = n_pts - 1 if z == 0 else n_pts
            for slots, recv, first, many in (
                (parts_a, a_recv, 0, rows_a), (parts_b, b_recv, rows_a, rows_b)
            ):
                t_col[...] = column_tile(top_row[...])[:TOPK, :]
                settle(slots.at[0, pl.ds(0, count)], recv.at[z])
                total = slots[z, 0]
                for p in range(1, n_pts):
                    total = total + slots[z, p]
                all_gains[z, first : first + many, :] = total
                top_row[...] = merge([total[t : t + 1, :] for t in range(many)])
            if z:
                @pl.when(speaks)
                def _():
                    for k in range(pair):
                        told(z, k, all_gains.at[z], got_gains, gain_send, gain_recv).start()
            if z == n_cand - 2:
                finish_cover()
                gains_out[...] = all_gains[0]
                settle(parts_a.at[0, pl.ds(0, n_pts - 1)], a_send.at[0])
                settle(parts_b.at[0, pl.ds(0, n_pts - 1)], b_send.at[0])
        top_out[...] = top_row[:, :TOPK]

        @pl.when(speaks)
        def _():
            for z in range(1, n_cand):
                for k in range(pair):
                    told(z, k, top_row, got_top, top_send, top_recv).start()
            many = pair * (n_cand - 1)
            for k in range(many):
                settle(got_gains, gain_send.at[0])
                settle(got_top, top_send.at[0])

    @pl.when(jnp.logical_not(base))
    def _():
        finish_cover()
        settle(parts_a.at[0, pl.ds(0, n_pts)], a_send.at[0])
        settle(parts_b.at[0, pl.ds(0, n_pts)], b_send.at[0])
        settle(got_gains, gain_recv.at[0])
        gains_out[...] = got_gains[...]
        settle(got_top, top_recv.at[0])
        top_out[...] = got_top[:, :TOPK]


def finish(gains, top, cover, gains_out, top_out, cover_out, sems):
    copies = [
        pltpu.make_async_copy(top, top_out, sems.at[0]),
        pltpu.make_async_copy(gains, gains_out, sems.at[1]),
        pltpu.make_async_copy(cover, cover_out, sems.at[2]),
    ]
    for copy in copies:
        copy.start()
    for copy in copies:
        copy.wait()


def solution(mesh):
    n_pts, n_cand = mesh.shape["pts"], mesh.shape["cand"]

    def on_device(points, weights, coverage, candidates, picks):
        rows, depth = points.shape
        cands = candidates.shape[0]
        tp, tc = rows // LANES, cands // LANES
        tb = WIDE // LANES
        ta = tc - tb
        anywhere = pl.BlockSpec(memory_space=pl.ANY)
        dma = pltpu.SemaphoreType.DMA
        vmem = pltpu.VMEM
        gains, top, cover = pl.pallas_call(
            functools.partial(kernel, n_pts, n_cand),
            out_shape=(vmem((tc, LANES), F32), vmem((1, TOPK), F32), vmem((tp, LANES), F32)),
            in_specs=[anywhere] * 5,
            out_specs=(pl.BlockSpec(memory_space=vmem),) * 3,
            scratch_shapes=[
                vmem((rows, depth), points.dtype), vmem((cands, depth), candidates.dtype),
                vmem((tp, LANES), F32), vmem((tp, LANES), F32),
                pltpu.SMEM(picks.shape, jnp.int32),
                vmem((rows, LANES), F32), vmem((rows, LANES), F32), vmem((rows, LANES), F32),
                vmem((ta, LANES), F32), vmem((tb, LANES), F32),
                vmem((n_cand, n_pts, ta, LANES), F32), vmem((n_cand, n_pts, tb, LANES), F32),
                vmem((tp, LANES), F32), vmem((n_cand, tp, LANES), F32),
                vmem((n_cand, tc, LANES), F32), vmem((cands, LANES), F32), vmem((TOPK, LANES), F32),
                vmem((1, LANES), F32), vmem((tc, LANES), F32), vmem((1, LANES), F32),
                dma((rows // HALF + cands // WIDE,)), dma((3,)),
                dma((1,)), dma((n_cand,)), dma((1,)), dma((n_cand,)), dma((1,)), dma((1,)),
                dma((1,)), dma((1,)), dma((1,)), dma((1,)),
                vmem((2 * (n_cand - 1), tc, LANES), F32),
            ],
            compiler_params=pltpu.CompilerParams(
                collective_id=0, has_side_effects=True, vmem_limit_bytes=60 * 2**20
            ),
            name="facility",
        )(points, weights.reshape(tp, LANES), coverage.reshape(tp, LANES), candidates, picks)
        gains, top, cover = pl.pallas_call(
            finish,
            out_shape=(
                jax.ShapeDtypeStruct((tc, LANES), F32),
                jax.ShapeDtypeStruct((1, TOPK), F32),
                jax.ShapeDtypeStruct((tp, LANES), F32),
            ),
            in_specs=[pl.BlockSpec(memory_space=vmem)] * 3,
            out_specs=(anywhere,) * 3,
            scratch_shapes=[dma((3,))],
            name="finish",
        )(*(pltpu.with_memory_space_constraint(x, vmem) for x in (gains, top, cover)))
        return gains.reshape(cands), top.reshape(TOPK), cover.reshape(rows)

    placed = (P("pts", None), P("pts"), P("pts"), P("cand", None), P())
    return jax.shard_map(
        on_device, mesh=mesh, in_specs=placed, out_specs=(P("cand"), P(), P("pts")), check_vma=False
    )
```

time: 17.2 us -> 18.8 us (1.093)
  the two profiles are of different devices: /device:TPU:0 before, /device:TPU:1 now
where the time goes in v1:
time: 18.8 us; the launch traced here: 18.6 us
  Pallas kernels  18 us (96%)
  between operations  0.64 us (3%)
    pallas_call x1, Pallas kernels, on_device(): pl.pallas_call(functools.partial(kernel, n_pts, n_cand), out_shape=(vmem(...  17.3 us
    pallas_call x1, Pallas kernels, on_device(): pl.pallas_call(finish, out_shape=(jax.ShapeDtypeStruct((tc, LANES), F32),...  0.63 us

profile of v1, /device:TPU:1, one launch (start us, length us, event | category | flops | bytes accessed | tf_op | source)
XLA Modules:
  0.0 18.6 jit_solution(1841545716938315805)
XLA Ops:
  0.6 17.3 %facility.1 = (f32[8,128]{1,0:T(8,128)S(1)}, f32[1,64]{1,0:T(1,128)S(1)}, f32[8,128]{1,0:T(8,128)S(1)}) custom-call(bf16[1024,1024]{1,0:T(8,128)(2,1)} %points.1, f32[8,128]{1,0:T(8,128)} %bitcast.5, f32[8,128]{1,0:T(8,128)} %bitcast.6, bf16[1024,1024]{1,0:T(8,128)(2,1)} %candidates.1, s32[64]{0:T(128)} %picks.1), custom_call_target="tpu_custom_call" | custom-call | tf_op jit(solution)/shard_map/facility/pallas_call | solution.py:285
  18.0 0.6 %finish.1 = (f32[8,128]{1,0:T(8,128)}, f32[1,64]{1,0:T(1,128)}, f32[8,128]{1,0:T(8,128)}) custom-call(f32[8,128]{1,0:T(8,128)S(1)} %get-tuple-element.9.gains, f32[1,64]{1,0:T(1,128)S(1)} %get-tuple-element.10.top, f32[8,128]{1,0:T(8,128)S(1)} %get-tuple-element.11.cover), custom_call_target="tpu_custom_call" | custom-call | tf_op jit(solution)/shard_map/finish/pallas_call | solution.py:310

commit v2 on v1

--- a/solution.py
+++ b/solution.py
@@ -13,9 +13,8 @@
 F32 = jnp.float32
 LOW = -1e30
 HIGH = 3e38
-HALF = 512
 WIDE = 256
-STEP = 64
+PIECE = 64
 
 
 def column_tile(row):
@@ -24,15 +23,17 @@
 
 def kernel(
     n_pts, n_cand, points, weights, coverage, candidates, picks, gains_out, top_out, cover_out,
-    p_buf, c_buf, w_buf, v_buf, k_buf, w_col, v_col, b_acc, part_a, part_b, parts_a, parts_b,
+    p_buf, c_buf, w_buf, v_buf, k_buf, w_col, v_col, b_acc, last, part_a, part_b, parts_a, parts_b,
     best, bests, all_gains, n_col, t_col, top_row, got_gains, got_top,
     in_sem, small_sem, a_send, a_recv, b_send, b_recv, best_send, best_recv,
-    gain_send, gain_recv, top_send, top_recv, sent,
+    gain_send, gain_recv, top_send, top_recv, *accs,
 ):
     rows, depth = points.shape
     cands = candidates.shape[0]
     me, mz = lax.axis_index("pts"), lax.axis_index("cand")
-    n_p, n_c = rows // HALF, cands // WIDE
+    n_k, n_c = depth // WIDE, cands // WIDE
+    half = rows // 2
+    pieces = half // PIECE
     tiles_p, tiles_c = rows // LANES, cands // LANES
     tiles_w = WIDE // LANES
     rows_b = tiles_w
@@ -40,20 +41,32 @@
     pair = 2 if n_pts % 2 == 0 else 1
     scale = depth ** (-0.5)
 
+    steps = [(c, k) for c in range(n_c) for k in range(n_k)]
+    order = [("c", steps[0])]
+    for at, step in enumerate(steps):
+        if at + 1 < len(steps):
+            order.append(("c", steps[at + 1]))
+        if step[0] == 0:
+            order.append(("p", step))
     loads = {}
-    order = [("c", 0), ("p", 0)] + [("p", i) for i in range(1, n_p)] + [("c", i) for i in range(1, n_c)]
-    for at, (kind, i) in enumerate(order):
-        src, dst, size = (points, p_buf, HALF) if kind == "p" else (candidates, c_buf, WIDE)
-        span = pl.ds(i * size, size)
-        loads[kind, i] = pltpu.make_async_copy(src.at[span, :], dst.at[span, :], in_sem.at[at])
+    for at, (kind, (c, k)) in enumerate(order):
+        side = pl.ds(k * WIDE, WIDE)
+        if kind == "p":
+            src, dst = points.at[:, side], p_buf.at[:, side]
+        else:
+            down = pl.ds(c * WIDE, WIDE)
+            src, dst = candidates.at[down, side], c_buf.at[down, side]
+        loads[kind, (c, k)] = pltpu.make_async_copy(src, dst, in_sem.at[at])
     small = [
         pltpu.make_async_copy(weights, w_buf, small_sem.at[0]),
         pltpu.make_async_copy(coverage, v_buf, small_sem.at[1]),
         pltpu.make_async_copy(picks, k_buf, small_sem.at[2]),
     ]
+    for key in order[:3]:
+        loads[key].start()
     for copy in small:
         copy.start()
-    for key in order:
+    for key in order[3:]:
         loads[key].start()
 
     base = mz == 0
@@ -93,77 +106,100 @@
         chosen = chosen | (column == k_buf[k])
     penalty = jnp.where(chosen, 0.0, LOW)
 
-    def dot(p_from, many, c):
-        return lax.dot_general(
-            p_buf[p_from : p_from + many, :], c_buf[c * WIDE : (c + 1) * WIDE, :],
-            (((1,), (1,)), ((), ())), preferred_element_type=F32,
-        )
-
-    def epilogue(sims, p_from, c, sums):
-        many = sims.shape[0]
-        for r in range(0, many, STEP):
-            at = slice(p_from + r, p_from + r + STEP)
-            w, v = w_col[at, :], v_col[at, :]
-            found = b_acc[at, :] if c else None
-            for t in range(tiles_w):
-                x = sims[r : r + STEP, t * LANES : (t + 1) * LANES]
-                value = jnp.maximum(x - v, 0.0) * w
-                value = jnp.sum(value.reshape(STEP // 8, 8, LANES), axis=0)
-                sums[t] = value if sums[t] is None else sums[t] + value
-                tile = c * tiles_w + t
-                x = x + penalty[tile : tile + 1, :]
-                found = x if found is None else jnp.maximum(found, x)
-            b_acc[at, :] = found
-
-    def settle_sums(sums, dst, c):
+    def push(at):
+        c, k = steps[at]
+        tile = c_buf[c * WIDE : (c + 1) * WIDE, k * WIDE : (k + 1) * WIDE]
+        for q in range(2):
+            pltpu.matmul_push_rhs(tile, staging_register=at % 2, mxu_index=q, transpose=True)
+
+    def accumulator(c, i, q):
+        return accs[((c % 2) * 2 + q) * pieces + i]
+
+    def accumulate(at):
+        c, k = steps[at]
+        for i in range(pieces):
+            for q in range(2):
+                from_p = q * half + i * PIECE
+                pltpu.matmul_acc_lhs(
+                    accumulator(c, i, q),
+                    p_buf[from_p : from_p + PIECE, k * WIDE : (k + 1) * WIDE],
+                    load_staged_rhs=at % 2 if i == 0 else None,
+                )
+
+    sums = {}
+
+    def gain_of(x, at, c, t):
+        value = jnp.maximum(x - v_col[at, :], 0.0) * w_col[at, :]
+        value = jnp.sum(value.reshape(PIECE // 8, 8, LANES), axis=0)
+        sums[c, t] = sums[c, t] + value if (c, t) in sums else value
+
+    def cover_of(xs, at, c):
+        found = b_acc[at, :] if c else None
+        for t, x in enumerate(xs):
+            tile = c * tiles_w + t
+            x = x + penalty[tile : tile + 1, :]
+            found = x if found is None else jnp.maximum(found, x)
+        b_acc[at, :] = found
+
+    def consume(c, i, q):
+        from_p = q * half + i * PIECE
+        at = slice(from_p, from_p + PIECE)
+        sims = pltpu.matmul_pop(accumulator(c, i, q))
+        xs = [sims[:, t * LANES : (t + 1) * LANES] for t in range(tiles_w)]
+        for t, x in enumerate(xs):
+            gain_of(x, at, c, t)
+        if c + 1 < n_c:
+            cover_of(xs, at, c)
+        else:
+            last[at, :] = sims
+
+    def write_sums(c, dst, row):
         for t in range(tiles_w):
-            dst[c * tiles_w + t : c * tiles_w + t + 1, :] = jnp.sum(sums[t], axis=0, keepdims=True)
+            dst[row + t : row + t + 1, :] = jnp.sum(sums[c, t], axis=0, keepdims=True)
 
     def send_parts(src, slots, send, recv):
-        def to(p):
-            pltpu.make_async_remote_copy(
+        slots[0, me] = src[...]
+        for k in range(n_pts):
+            p = k + jnp.where(base & (k >= me), 1, 0)
+            copy = pltpu.make_async_remote_copy(
                 src_ref=src, dst_ref=slots.at[mz, me], send_sem=send.at[0], recv_sem=recv.at[mz],
                 device_id={"pts": p, "cand": 0}, device_id_type=MESH,
-            ).start()
-
-        @pl.when(jnp.logical_not(base))
-        def _():
-            for p in range(n_pts):
-                to(p)
-
-        @pl.when(base)
-        def _():
-            for k in range(1, n_pts):
-                to(lax.rem(me + k, n_pts))
-            slots[0, me] = src[...]
-
-    work = []
-    for i in range(n_p):
-        work.append((i * HALF, HALF, 0, ("p", i)))
-    for c in range(1, n_c):
-        work.append((0, rows, c, ("c", c)))
-    loads["c", 0].wait()
-    sums = [None] * tiles_w
-    held = None
-    for at, (p_from, many, c, key) in enumerate(work):
-        loads[key].wait()
-        sims = dot(p_from, many, c)
-        if held is not None:
-            epilogue(*held, sums)
-            if held[2] != c:
-                settle_sums(sums, part_a, held[2])
-                sums = [None] * tiles_w
-        held = (sims, p_from, c)
+            )
+            if k + 1 < n_pts:
+                copy.start()
+            else:
+                pl.when(jnp.logical_not(base))(copy.start)
+
+    loads["c", steps[0]].wait()
+    push(0)
+    units = [(i, q) for i in range(pieces) for q in range(2)]
+    share = len(units) // n_k
+    for at, (c, k) in enumerate(steps):
+        if c == 0:
+            loads["p", (c, k)].wait()
+        if at + 1 < len(steps):
+            loads["c", steps[at + 1]].wait()
+            push(at + 1)
+        accumulate(at)
+        if c:
+            for i, q in units[k * share : (k + 1) * share]:
+                consume(c - 1, i, q)
+            if k == n_k - 1:
+                write_sums(c - 1, part_a, (c - 1) * tiles_w)
 
     greetings = (n_cand - 1) + n_pts
     awaited = jnp.where(base, greetings - 1, greetings)
     awaited = awaited + jnp.where(speaks, pair * (n_cand - 1), 0)
     pl.semaphore_wait(barrier, awaited)
     send_parts(part_a, parts_a, a_send, a_recv)
-    epilogue(*held, sums)
-    settle_sums(sums, part_b, 0)
+    for i, q in units:
+        consume(n_c - 1, i, q)
+    write_sums(n_c - 1, part_b, 0)
     send_parts(part_b, parts_b, b_send, b_recv)
 
+    for r in range(0, rows, PIECE):
+        at = slice(r, r + PIECE)
+        cover_of([last[at, t * LANES : (t + 1) * LANES] for t in range(tiles_w)], at, n_c - 1)
     for t in range(tiles_p):
         turned = jnp.transpose(b_acc[t * LANES : (t + 1) * LANES, :])
         best[t : t + 1, :] = jnp.max(turned, axis=0, keepdims=True)
@@ -282,8 +318,14 @@
         anywhere = pl.BlockSpec(memory_space=pl.ANY)
         dma = pltpu.SemaphoreType.DMA
         vmem = pltpu.VMEM
+
+        def scoped(*refs):
+            many = rows // 2 // PIECE
+            accs = [pltpu.ACC(q)((PIECE, WIDE), F32) for q in (0,) * many + (1,) * many] * 2
+            pl.run_scoped(functools.partial(kernel, n_pts, n_cand, *refs), *accs)
+
         gains, top, cover = pl.pallas_call(
-            functools.partial(kernel, n_pts, n_cand),
+            scoped,
             out_shape=(vmem((tc, LANES), F32), vmem((1, TOPK), F32), vmem((tp, LANES), F32)),
             in_specs=[anywhere] * 5,
             out_specs=(pl.BlockSpec(memory_space=vmem),) * 3,
@@ -292,15 +334,15 @@
                 vmem((tp, LANES), F32), vmem((tp, LANES), F32),
                 pltpu.SMEM(picks.shape, jnp.int32),
                 vmem((rows, LANES), F32), vmem((rows, LANES), F32), vmem((rows, LANES), F32),
+                vmem((rows, WIDE), F32),
                 vmem((ta, LANES), F32), vmem((tb, LANES), F32),
                 vmem((n_cand, n_pts, ta, LANES), F32), vmem((n_cand, n_pts, tb, LANES), F32),
                 vmem((tp, LANES), F32), vmem((n_cand, tp, LANES), F32),
                 vmem((n_cand, tc, LANES), F32), vmem((cands, LANES), F32), vmem((TOPK, LANES), F32),
                 vmem((1, LANES), F32), vmem((tc, LANES), F32), vmem((1, LANES), F32),
-                dma((rows // HALF + cands // WIDE,)), dma((3,)),
+                dma(((depth // WIDE) * (cands // WIDE + 1),)), dma((3,)),
                 dma((1,)), dma((n_cand,)), dma((1,)), dma((n_cand,)), dma((1,)), dma((1,)),
                 dma((1,)), dma((1,)), dma((1,)), dma((1,)),
-                vmem((2 * (n_cand - 1), tc, LANES), F32),
             ],
             compiler_params=pltpu.CompilerParams(
                 collective_id=0, has_side_effects=True, vmem_limit_bytes=60 * 2**20

time: 18.8 us -> 16.2 us (0.86)
  Pallas kernels: 18 us -> 15.4 us
    pallas_call x1, Pallas kernels: 17.3 us -> 14.8 us  [on_device(): pl.pallas_call(scoped, out_shape=(vmem((tc, LANES), F32), vmem((1, TOPK),...]
where the time goes in v2:
time: 16.2 us; the launch traced here: 16.1 us
  Pallas kernels  15.4 us (95%)
  between operations  0.64 us (4%)
    pallas_call x1, Pallas kernels, on_device(): pl.pallas_call(scoped, out_shape=(vmem((tc, LANES), F32), vmem((1, TOPK),...  14.8 us
    pallas_call x1, Pallas kernels, on_device(): pl.pallas_call(finish, out_shape=(jax.ShapeDtypeStruct((tc, LANES), F32),...  0.63 us

profile of v2, /device:TPU:1, one launch (start us, length us, event | category | flops | bytes accessed | tf_op | source)
XLA Modules:
  0.0 16.1 jit_solution(8106359775429738043)
XLA Ops:
  0.6 14.8 %facility.1 = (f32[8,128]{1,0:T(8,128)S(1)}, f32[1,64]{1,0:T(1,128)S(1)}, f32[8,128]{1,0:T(8,128)S(1)}) custom-call(bf16[1024,1024]{1,0:T(8,128)(2,1)} %refs_0_.1, f32[8,128]{1,0:T(8,128)} %bitcast.5, f32[8,128]{1,0:T(8,128)} %bitcast.6, bf16[1024,1024]{1,0:T(8,128)(2,1)} %refs_3_.1, s32[64]{0:T(128)} %refs_4_.1), custom_call_target="tpu_custom_call" | custom-call | tf_op jit(solution)/shard_map/facility/pallas_call | solution.py:327
  15.4 0.6 %finish.1 = (f32[8,128]{1,0:T(8,128)}, f32[1,64]{1,0:T(1,128)}, f32[8,128]{1,0:T(8,128)}) custom-call(f32[8,128]{1,0:T(8,128)S(1)} %get-tuple-element.9.gains, f32[1,64]{1,0:T(1,128)S(1)} %get-tuple-element.10.top, f32[8,128]{1,0:T(8,128)S(1)} %get-tuple-element.11.cover), custom_call_target="tpu_custom_call" | custom-call | tf_op jit(solution)/shard_map/finish/pallas_call | solution.py:352
